TPU v7x, 32 devices: a whole 2x2x4 slice. The times are simulated.
32 devices in a mesh: row: 8 (over y, x, core), col: 4 (over z).
Axes of the slice: x: 2, y: 2, z: 4, core: 2. Of those that a mesh axis runs over, the one named last changes fastest.
Arguments:
- acts: bfloat16 [512, 16384], P('row', 'col'), may hold values from -6 to 6
- grads: float32 [16384, 512], P('col', 'row'), may hold values from -24 to 24
Outputs:
- factor: float32 [16384, 16384], P('row', 'col')
- applied: float32 [16384, 512], P('row', 'col')
- solution: float32 [16384, 512], P('col', 'row')
All inputs are finite; a program needn't handle non-finite values.
Results may differ from a plain program's by a relative error of at most 0.0003.
Values may be sent and summed in bfloat16 or wider, within the bound.
No kernel may reach another device: no remote copies, remote signals or barrier semaphores. Data moves between devices by JAX's collectives and lax.ppermute only.
A program may use at most 128 MiB of HBM per device.

v0:
```python
import math
import jax
import jax.numpy as jnp
from jax import lax
from jax.sharding import PartitionSpec as P

damping = 1.0
highest = lax.Precision.HIGHEST


def from_root(value, axis, source):
    kept = jnp.where(lax.axis_index(axis) == source, value, 0).astype(value.dtype)
    return lax.psum(kept, axis)


def step_size(feature_count, token_count):
    return 1.0 / (damping + (1.0 + math.sqrt(feature_count / token_count)) ** 2)


def local(acts, grads):
    row_count = lax.axis_size("row")
    col_count = lax.axis_size("col")
    row_ratio = row_count // col_count
    row_index = lax.axis_index("row")
    col_index = lax.axis_index("col")
    outer_width = acts.shape[1]
    inner_width = outer_width // row_ratio
    token_count = acts.shape[0] * row_count
    omega_step = step_size(outer_width * col_count, token_count)
    row_offset = row_index % row_ratio * inner_width
    owner_col = row_index // row_ratio
    column_panel = lax.all_gather(acts, "row", axis=0, tiled=True)
    owned_slice = lax.dynamic_slice_in_dim(column_panel, row_offset, inner_width, 1)
    inner_panel = from_root(owned_slice, "col", owner_col)
    gram_sum = lax.dot_general(
        inner_panel, column_panel, (((0,), (0,)), ((), ())), preferred_element_type=jnp.float32
    )
    gram_tile = gram_sum / token_count
    is_owner = (col_index == owner_col).astype(jnp.float32)
    gathered = lax.all_gather(grads, "row", axis=1, tiled=True)
    mirror_rows = lax.dynamic_slice_in_dim(gathered, row_offset, inner_width, 0)
    partial_sum = jnp.dot(gram_tile, gathered, precision=highest) + damping * is_owner * mirror_rows
    full_applied = lax.psum(partial_sum, "col")
    share = full_applied.shape[1] // col_count
    applied = lax.dynamic_slice_in_dim(full_applied, col_index * share, share, 1)
    mirror_coef = omega_step**3 * damping - 3.0 * omega_step**2
    empty_block = jnp.zeros((outer_width, full_applied.shape[1]), jnp.float32)
    placed = lax.dynamic_update_slice_in_dim(
        empty_block, full_applied * (mirror_coef * is_owner), row_offset, 0
    )
    second_sum = (
        omega_step**3
        * lax.dot_general(
            gram_tile,
            full_applied,
            (((0,), (0,)), ((), ())),
            precision=highest,
            preferred_element_type=jnp.float32,
        )
        + placed
    )
    solution = 3.0 * omega_step * grads + lax.psum_scatter(
        second_sum, "row", scatter_dimension=1, tiled=True
    )
    return (gram_tile, applied, solution)


def solution(mesh):
    in_specs = (P("row", "col"), P("col", "row"))
    out_specs = (P("row", "col"), P("row", "col"), P("col", "row"))
    return jax.shard_map(local, mesh=mesh, in_specs=in_specs, out_specs=out_specs, check_vma=False)
```

profile of v0, /device:TPU:0, one launch (start us, length us, event | category | flops | bytes accessed | tf_op | source)
XLA Modules:
  0.0 583.2 jit_solution(10916674862800319205)
XLA Ops:
  7.2 0.0 all-gather.3.cloned.1.call-start
  7.2 0.7 all-gather.3.cloned.1.call-update
  7.9 0.0 all-reduce.3.cloned.1.call-start
  8.0 41.2 %all-gather.3.cloned.1.call-done = bf16[512,4096]{1,0:T(8,128)(2,1)} async-done(((bf16[64,4096]{1,0:T(8,128)(2,1)}), bf16[512,4096]{1,0:T(8,128)(2,1)}) %all-gather.3.cloned.1.call-update) | async-done | bytes 4194320 | tf_op jit(solution)/shard_map/all_gather | solution.py:32
  49.2 3.4 dynamic-slice_select_fusion
  52.6 0.0 all-reduce.3.cloned.1.call-update
  52.7 0.0 all-gather.5.cloned.1.call-start
  52.7 0.7 all-gather.5.cloned.1.call-update
  53.4 0.0 all-reduce.5.cloned.1.call-start
  53.5 85.5 %all-reduce.3.cloned.1.call-done = bf16[512,2048]{1,0:T(8,128)(2,1)} async-done(((bf16[512,2048]{1,0:T(8,128)(2,1)}), bf16[512,2048]{1,0:T(8,128)(2,1)}) %all-reduce.3.cloned.1.call-update) | async-done | bytes 2097168 | tf_op jit(solution)/shard_map/psum | solution.py:13
  139.0 18.8 %convolution_multiply_fusion = f32[2048,4096]{1,0:T(8,128)} fusion(bf16[512,2048]{1,0:T(8,128)(2,1)} %all-reduce.3.cloned.1.call-done, bf16[512,4096]{1,0:T(8,128)(2,1)} %all-gather.3.cloned.1.call-done), kind=kOutput, calls=%fused_computation | convolution fusion | flops 8598323200 | bytes 39845888 | tf_op jit(solution)/shard_map/dot_general | solution.py:35
  157.7 36.5 %all-gather.5.cloned.1.call-done = f32[4096,512]{0,1:T(8,128)} async-done(((f32[4096,64]{0,1:T(8,128)}), f32[4096,512]{0,1:T(8,128)}) %all-gather.5.cloned.1.call-update) | async-done | bytes 8388624 | tf_op jit(solution)/shard_map/all_gather | solution.py:40
  194.2 4.6 constant_dynamic-slice_fusion.1
  198.8 5.3 copy.13
  204.2 62.2 %multiply_add_fusion = f32[2048,512]{1,0:T(8,128)} fusion(f32[2048,512]{1,0:T(8,128)} %copy.13, f32[2048,4096]{1,0:T(8,128)} %convolution_multiply_fusion, f32[4096,512]{0,1:T(8,128)} %all-gather.5.cloned.1.call-done, f32[]{:T(128)S(6)} %convert_element_type.5), kind=kOutput, calls=%fused_computation.3 | convolution fusion | flops 51541704704 | bytes 50331652 | tf_op jit(solution)/shard_map/dot_general | solution.py:42
  266.3 0.0 all-reduce.5.cloned.1.call-update
  266.4 0.0 reduce-scatter.4.cloned.1.call-start
  266.4 155.1 %all-reduce.5.cloned.1.call-done = f32[2048,512]{1,0:T(8,128)} async-done(((f32[2048,512]{1,0:T(8,128)}), f32[2048,512]{1,0:T(8,128)}) %all-reduce.5.cloned.1.call-update) | async-done | bytes 4194320 | tf_op jit(solution)/shard_map/psum | solution.py:43
  421.5 0.0 copy-start
  421.5 60.8 %convolution_multiply_fusion.1 = f32[4096,512]{1,0:T(8,128)} fusion(f32[2048,4096]{1,0:T(8,128)} %convolution_multiply_fusion, f32[2048,512]{1,0:T(8,128)} %all-reduce.5.cloned.1.call-done), kind=kOutput, calls=%fused_computation.1 | convolution fusion | flops 51541704704 | bytes 46137344 | tf_op jit(solution)/shard_map/dot_general | solution.py:53
  482.3 0.0 copy-done
  482.3 5.2 add_dynamic-update-slice_fusion
  487.5 9.0 %copy.11 = f32[4096,512]{0,1:T(8,128)} copy(f32[4096,512]{1,0:T(8,128)} %add_dynamic-update-slice_fusion) | data formatting | bytes 16777216
  496.5 0.0 copy-start.1
  496.5 0.0 reduce-scatter.4.cloned.1.call-update
  496.5 1.2 copy-done.1
  497.7 0.6 copy.9
  498.3 2.3 constant_dynamic-slice_fusion
  500.6 66.6 %reduce-scatter.4.cloned.1.call-done = f32[64,4096]{1,0:T(8,128)} async-done(((f32[512,4096]{1,0:T(8,128)}), f32[64,4096]{1,0:T(8,128)}) %reduce-scatter.4.cloned.1.call-update) | async-done | bytes 1048592
  567.2 3.2 copy.12
  570.4 3.2 multiply_add_fusion.1
  573.5 3.1 copy.10
Async XLA Ops:
  7.2 42.0 %all-gather.3.cloned.1.call-start = ((), (), s32[]{:S(2)}) async-start(), calls=%async_computation.1 | async-start | bytes 4718592 | tf_op jit(solution)/shard_map/all_gather | solution.py:32
  7.9 131.1 %all-reduce.3.cloned.1.call-start = ((), (), s32[]{:S(2)}) async-start(), calls=%async_computation.2 | async-start | bytes 4194304 | tf_op jit(solution)/shard_map/psum | solution.py:13
  52.7 141.5 %all-gather.5.cloned.1.call-start = ((), (), s32[]{:S(2)}) async-start(), calls=%async_computation.3 | async-start | bytes 9437184 | tf_op jit(solution)/shard_map/all_gather | solution.py:40
  53.4 368.1 %all-reduce.5.cloned.1.call-start = ((), (), s32[]{:S(2)}) async-start(), calls=%async_computation.4 | async-start | bytes 8388608 | tf_op jit(solution)/shard_map/psum | solution.py:43
  266.4 300.8 %reduce-scatter.4.cloned.1.call-start = ((), (), s32[]{:S(2)}) async-start(), calls=%async_computation.5 | async-start | bytes 9437184
  421.5 60.8 %copy-start = (f32[2048,512]{1,0:T(8,128)S(1)}, f32[2048,512]{1,0:T(8,128)}, u32[]{:S(2)}) copy-start(f32[2048,512]{1,0:T(8,128)} %all-reduce.5.cloned.1.call-done) | copy-start | bytes 12582916
  496.5 1.2 copy-start.1
Sparse Core Ops, SparseCore 0:
  9.9 39.2 all-gather.2
  52.8 86.1 all-reduce.2
  140.9 53.2 all-gather.4
  266.5 154.9 all-reduce.4
  496.7 70.4 reduce-scatter.3
where the time goes:
time: 584 us; the launch traced here: 583 us
  waiting for transfers between devices  386 us (66%)
  matrix products  142 us (24%)
  local copies, waits for them, and re-layouts  29.4 us (5%)
  between operations  13.8 us (2%)
  other arithmetic  11.8 us (2%)
    psum x1, waiting for transfers between devices, local(): full_applied = lax.psum(partial_sum, 'col')  155 us
    psum x1, waiting for transfers between devices, from_root(): return lax.psum(kept, axis)  85.5 us
    unnamed x6, waiting for transfers between devices  68 us
    dot_general x1, matrix products, local(): jnp.dot(gram_tile, gathered, precision=highest)  62.2 us
    dot_general x1, matrix products, local(): lax.dot_general(gram_tile, full_applied, (((0,), (0,)), ((), ())), precis...  60.8 us
    all_gather x1, waiting for transfers between devices, local(): column_panel = lax.all_gather(acts, 'row', axis=0, tiled=True)  41.2 us
    all_gather x1, waiting for transfers between devices, local(): gathered = lax.all_gather(grads, 'row', axis=1, tiled=True)  36.5 us
    unnamed x9, local copies, waits for them, and re-layouts  22.5 us
  transfers between devices with their start and end apart: 5, of which 5 were waited for; matrix products, arithmetic and copies ran while one was open for 4% of the time, Pallas kernels for 0%

commit v1 on v0

--- a/solution.py
+++ b/solution.py
@@ -6,11 +6,12 @@
 
 damping = 1.0
 highest = lax.Precision.HIGHEST
+remake_targets_by_axis = lambda raw, axis_tag: jnp.sum(jax.lax.all_gather(raw, axis_tag), 0)
 
 
 def from_root(value, axis, source):
     kept = jnp.where(lax.axis_index(axis) == source, value, 0).astype(value.dtype)
-    return lax.psum(kept, axis)
+    return remake_targets_by_axis(kept, axis)
 
 
 def step_size(feature_count, token_count):

time: 584 us -> 657 us (1.12)
  waiting for transfers between devices: 386 us -> 455 us
    all_gather x0 -> x1, waiting for transfers between devices: none -> 141 us  [jax.lax.all_gather(raw, axis_tag)]
    psum x1 -> x0, waiting for transfers between devices: 85.5 us -> none  [from_root(): return lax.psum(kept, axis)]
    all_gather x1, waiting for transfers between devices: 36.5 us -> 52.6 us  [local(): gathered = lax.all_gather(grads, 'row', axis=1, tiled=True)]
    unnamed x9 -> x11, local copies, waits for them, and re-layouts: 22.5 us -> 22.5 us
  transfers between devices with their start and end apart: 5 -> 5, of which waited for: 5 -> 5; matrix products, arithmetic and copies ran while one was open for 4% -> 3% of each run, Pallas kernels for 0% -> 0%
where the time goes in v1:
time: 657 us
  waiting for transfers between devices  455 us (69%)
  matrix products  140 us (21%)
  local copies, waits for them, and re-layouts  29.4 us (4%)
  other arithmetic  17.5 us (3%)
  between operations  13.9 us (2%)
    psum x1, waiting for transfers between devices, local(): full_applied = lax.psum(partial_sum, 'col')  153 us
    all_gather x1, waiting for transfers between devices, jax.lax.all_gather(raw, axis_tag)  141 us
    unnamed x6, waiting for transfers between devices  68 us
    dot_general x1, matrix products, local(): jnp.dot(gram_tile, gathered, precision=highest)  60.8 us
    dot_general x1, matrix products, local(): lax.dot_general(gram_tile, full_applied, (((0,), (0,)), ((), ())), precis...  60.8 us
    all_gather x1, waiting for transfers between devices, local(): gathered = lax.all_gather(grads, 'row', axis=1, tiled=True)  52.6 us
    all_gather x1, waiting for transfers between devices, local(): column_panel = lax.all_gather(acts, 'row', axis=0, tiled=True)  40.5 us
    unnamed x11, local copies, waits for them, and re-layouts  22.5 us
  transfers between devices with their start and end apart: 5, of which 5 were waited for; matrix products, arithmetic and copies ran while one was open for 3% of the time, Pallas kernels for 0%

profile of v1, /device:TPU:0, one launch (start us, length us, event | category | flops | bytes accessed | tf_op | source)
XLA Modules:
  0.0 656.7 jit_solution(17399756839932077292)
XLA Ops:
  7.2 0.0 all-gather.5.cloned.1.call-start
  7.2 0.7 all-gather.5.cloned.1.call-update
  7.9 0.0 all-gather.7.cloned.1.call-start
  7.9 0.7 all-gather.7.cloned.1.call-update
  8.6 0.0 all-gather.9.cloned.1.call-start
  8.7 40.5 %all-gather.5.cloned.1.call-done = bf16[512,4096]{1,0:T(8,128)(2,1)} async-done(((bf16[64,4096]{1,0:T(8,128)(2,1)}), bf16[512,4096]{1,0:T(8,128)(2,1)}) %all-gather.5.cloned.1.call-update) | async-done | bytes 4194320 | tf_op jit(solution)/shard_map/all_gather | solution.py:33
  49.2 3.5 dynamic-slice_select_fusion
  52.7 0.0 all-gather.9.cloned.1.call-update
  52.7 0.0 all-reduce.2.cloned.1.call-start
  52.8 52.6 %all-gather.7.cloned.1.call-done = f32[4096,512]{0,1:T(8,128)} async-done(((f32[4096,64]{0,1:T(8,128)}), f32[4096,512]{0,1:T(8,128)}) %all-gather.7.cloned.1.call-update) | async-done | bytes 8388624 | tf_op jit(solution)/shard_map/all_gather | solution.py:41
  105.4 4.7 constant_dynamic-slice_fusion.1
  110.1 5.4 copy.13
  115.5 141.1 %all-gather.9.cloned.1.call-done = bf16[2048,2048]{1,0:T(8,128)(2,1)} async-done(((bf16[512,2048]{1,0:T(8,128)(2,1)}), bf16[2048,2048]{1,0:T(8,128)(2,1)}) %all-gather.9.cloned.1.call-update) | async-done | bytes 8388624 | tf_op jit(solution)/shard_map/all_gather | solution.py:9
  256.6 5.7 reduce_sum.12
  262.3 0.0 copy-start.2
  262.3 18.6 %convolution_multiply_fusion = f32[2048,4096]{1,0:T(8,128)} fusion(bf16[512,2048]{1,0:T(8,128)(2,1)S(1)} %reduce_sum.12, bf16[512,4096]{1,0:T(8,128)(2,1)} %all-gather.5.cloned.1.call-done), kind=kOutput, calls=%fused_computation | convolution fusion | flops 8598323200 | bytes 39845888 | tf_op jit(solution)/shard_map/dot_general | solution.py:36
  280.9 0.0 copy-done.2
  280.9 60.8 %multiply_add_fusion = f32[2048,512]{1,0:T(8,128)} fusion(f32[2048,512]{1,0:T(8,128)S(1)} %copy-done.2, f32[2048,4096]{1,0:T(8,128)} %convolution_multiply_fusion, f32[4096,512]{0,1:T(8,128)} %all-gather.7.cloned.1.call-done, f32[]{:T(128)S(6)} %convert_element_type.4), kind=kOutput, calls=%fused_computation.3 | convolution fusion | flops 51541704704 | bytes 50331652 | tf_op jit(solution)/shard_map/dot_general | solution.py:43
  341.7 0.0 all-reduce.2.cloned.1.call-update
  341.8 0.0 reduce-scatter.4.cloned.1.call-start
  341.8 153.3 %all-reduce.2.cloned.1.call-done = f32[2048,512]{1,0:T(8,128)} async-done(((f32[2048,512]{1,0:T(8,128)}), f32[2048,512]{1,0:T(8,128)}) %all-reduce.2.cloned.1.call-update) | async-done | bytes 4194320 | tf_op jit(solution)/shard_map/psum | solution.py:44
  495.1 0.0 copy-start
  495.1 60.8 %convolution_multiply_fusion.1 = f32[4096,512]{1,0:T(8,128)} fusion(f32[2048,4096]{1,0:T(8,128)} %convolution_multiply_fusion, f32[2048,512]{1,0:T(8,128)} %all-reduce.2.cloned.1.call-done), kind=kOutput, calls=%fused_computation.1 | convolution fusion | flops 51541704704 | bytes 46137344 | tf_op jit(solution)/shard_map/dot_general | solution.py:54
  555.9 0.0 copy-done
  555.9 5.2 add_dynamic-update-slice_fusion
  561.1 8.9 %copy.11 = f32[4096,512]{0,1:T(8,128)} copy(f32[4096,512]{1,0:T(8,128)} %add_dynamic-update-slice_fusion) | data formatting | bytes 16777216
  570.0 0.0 copy-start.1
  570.0 0.0 reduce-scatter.4.cloned.1.call-update
  570.0 1.2 copy-done.1
  571.2 0.6 copy.9
  571.8 2.3 constant_dynamic-slice_fusion
  574.1 66.6 %reduce-scatter.4.cloned.1.call-done = f32[64,4096]{1,0:T(8,128)} async-done(((f32[512,4096]{1,0:T(8,128)}), f32[64,4096]{1,0:T(8,128)}) %reduce-scatter.4.cloned.1.call-update) | async-done | bytes 1048592
  640.7 3.2 copy.12
  643.9 3.2 multiply_add_fusion.1
  647.0 3.1 copy.10
Async XLA Ops:
  7.2 42.0 %all-gather.5.cloned.1.call-start = ((), (), s32[]{:S(2)}) async-start(), calls=%async_computation.1 | async-start | bytes 4718592 | tf_op jit(solution)/shard_map/all_gather | solution.py:33
  7.9 97.5 %all-gather.7.cloned.1.call-start = ((), (), s32[]{:S(2)}) async-start(), calls=%async_computation.2 | async-start | bytes 9437184 | tf_op jit(solution)/shard_map/all_gather | solution.py:41
  8.6 247.9 %all-gather.9.cloned.1.call-start = ((), (), s32[]{:S(2)}) async-start(), calls=%async_computation.4 | async-start | bytes 10485760 | tf_op jit(solution)/shard_map/all_gather | solution.py:9
  52.7 442.4 %all-reduce.2.cloned.1.call-start = ((), (), s32[]{:S(2)}) async-start(), calls=%async_computation.3 | async-start | bytes 8388608 | tf_op jit(solution)/shard_map/psum | solution.py:44
  262.3 18.6 %copy-start.2 = (f32[2048,512]{1,0:T(8,128)S(1)}, f32[2048,512]{1,0:T(8,128)}, u32[]{:S(2)}) copy-start(f32[2048,512]{1,0:T(8,128)} %copy.13) | copy-start | bytes 12582916
  341.8 298.9 %reduce-scatter.4.cloned.1.call-start = ((), (), s32[]{:S(2)}) async-start(), calls=%async_computation.5 | async-start | bytes 9437184
  495.1 60.8 %copy-start = (f32[2048,512]{1,0:T(8,128)S(1)}, f32[2048,512]{1,0:T(8,128)}, u32[]{:S(2)}) copy-start(f32[2048,512]{1,0:T(8,128)} %all-reduce.2.cloned.1.call-done) | copy-start | bytes 12582916
  570.0 1.2 copy-start.1
Sparse Core Ops, SparseCore 0:
  9.9 39.2 all-gather.4
  51.1 54.2 all-gather.6
  107.0 149.5 all-gather.8
  341.9 153.1 all-reduce.1
  570.2 70.4 reduce-scatter.3
